TPU v7x, 8 devices: a whole 2x2x1 slice. The times are simulated.
8 devices in a mesh: replica: 2 (over z, y), model: 4 (over x, core).
Axes of the slice: x: 2, y: 2, z: 1, core: 2. Of those that a mesh axis runs over, the one named last changes fastest.
Arguments:
- tokens: bfloat16 [256, 3072], P('replica'), parts along dimension 0
- lengths: int32 [256], P('replica'), parts along dimension 0
- k_cache: bfloat16 [256, 8, 512, 128], P('replica'), parts along dimension 0
- v_cache: bfloat16 [256, 8, 512, 128], P('replica'), parts along dimension 0
- norm_gain: bfloat16 [3072], replicated
- w_query: bfloat16 [3072, 3072], P(None, 'model')
- w_key: bfloat16 [3072, 1024], replicated
- w_value: bfloat16 [3072, 1024], replicated
- w_out: bfloat16 [3072, 3072], P('model')
- w_gate: bfloat16 [3072, 12288], P(None, 'model')
- w_up: bfloat16 [3072, 12288], P(None, 'model')
- w_down: bfloat16 [12288, 3072], P('model')
Outputs:
- output 1: bfloat16 [256, 3072], P('replica'), parts along dimension 0
- output 2: bfloat16 [256, 8, 128], P(('replica', 'model')), parts along dimension 0
- output 3: bfloat16 [256, 8, 128], P(('replica', 'model')), parts along dimension 0
There are 2 independent parts. A program takes and returns all parts, laid end to end along the dimension named above; an argument that names none is the same for every part.
All inputs are finite; a program needn't handle non-finite values.
Results may differ from a plain program's by a relative error of at most 0.00484794.
Values are sent between devices in bfloat16 or wider.
A program may use at most 1.5 GiB of HBM per device.

v0:
```python
import math
import jax
import jax.numpy as jnp
from jax import lax
from jax.sharding import PartitionSpec as P

ROPE_BASE = 10000.0
NORM_EPS = 1e-6
MASK_VALUE = -1e30


def rms_norm(tokens, norm_gain):
    values = tokens.astype(jnp.float32)
    mean_sq = jnp.mean(values * values, axis=-1, keepdims=True)
    return (values * lax.rsqrt(mean_sq + NORM_EPS) * norm_gain.astype(jnp.float32)).astype(jnp.bfloat16)


def apply_rope(values, positions):
    half_dim = values.shape[-1] // 2
    inv_freq = jnp.exp(jnp.arange(half_dim, dtype=jnp.float32) * (-2.0 * math.log(ROPE_BASE) / values.shape[-1]))
    angles = positions.astype(jnp.float32)[:, None, None] * inv_freq[None, None, :]
    cos_part = jnp.cos(angles)
    sin_part = jnp.sin(angles)
    first_half = values[..., :half_dim]
    second_half = values[..., half_dim:]
    return jnp.concatenate([first_half * cos_part - second_half * sin_part, second_half * cos_part + first_half * sin_part], axis=-1)


def attend(queries, key_rows, value_rows, key_new, value_new, row_lengths):
    row_count, heads, head_dim = queries.shape
    kv_heads = key_rows.shape[1]
    grouped = queries.reshape(row_count, kv_heads, heads // kv_heads, head_dim)
    scale = head_dim ** -0.5
    scores = jnp.einsum('bgrd,bgtd->bgrt', grouped, key_rows, preferred_element_type=jnp.float32) * scale
    valid = jnp.arange(key_rows.shape[2])[None, None, None, :] < row_lengths[:, None, None, None]
    scores = jnp.where(valid, scores, MASK_VALUE)
    score_new = jnp.einsum('bgrd,bgd->bgr', grouped, key_new, preferred_element_type=jnp.float32) * scale
    peak = jnp.maximum(jnp.max(scores, axis=-1), score_new)
    weights = jnp.exp(scores - peak[..., None])
    weight_new = jnp.exp(score_new - peak)
    total = jnp.sum(weights, axis=-1) + weight_new
    mixed = jnp.einsum('bgrt,bgtd->bgrd', weights.astype(jnp.bfloat16), value_rows, preferred_element_type=jnp.float32)
    mixed = mixed + weight_new.astype(jnp.bfloat16).astype(jnp.float32)[..., None] * value_new.astype(jnp.float32)[:, :, None, :]
    return (mixed / total[..., None]).astype(jnp.bfloat16).reshape(row_count, heads, head_dim)


def solution(mesh):
    groups = mesh.shape['model']

    def local_step(tokens, lengths, k_cache, v_cache, norm_gain, w_query, w_key, w_value, w_out, w_gate, w_up, w_down):
        batch = tokens.shape[0]
        kv_heads = k_cache.shape[1]
        head_dim = k_cache.shape[3]
        local_heads = w_query.shape[1] // head_dim
        row_count = batch // groups
        row_start = lax.axis_index('model') * row_count
        normed = rms_norm(tokens, norm_gain)
        queries = apply_rope(jnp.dot(normed, w_query, preferred_element_type=jnp.float32).reshape(batch, local_heads, head_dim), lengths).astype(jnp.bfloat16)
        queries = lax.all_to_all(queries, 'model', 0, 1, tiled=True)
        row_lengths = lax.dynamic_slice_in_dim(lengths, row_start, row_count)
        row_normed = lax.dynamic_slice_in_dim(normed, row_start, row_count)
        key_new = apply_rope(jnp.dot(row_normed, w_key, preferred_element_type=jnp.float32).reshape(row_count, kv_heads, head_dim), row_lengths).astype(jnp.bfloat16)
        value_new = jnp.dot(row_normed, w_value, preferred_element_type=jnp.float32).reshape(row_count, kv_heads, head_dim).astype(jnp.bfloat16)
        key_rows = lax.dynamic_slice_in_dim(k_cache, row_start, row_count)
        value_rows = lax.dynamic_slice_in_dim(v_cache, row_start, row_count)
        attended = attend(queries, key_rows, value_rows, key_new, value_new, row_lengths)
        attended = lax.all_to_all(attended, 'model', 1, 0, tiled=True)
        hidden = (jax.nn.silu(jnp.dot(normed, w_gate, preferred_element_type=jnp.float32)) * jnp.dot(normed, w_up, preferred_element_type=jnp.float32)).astype(jnp.bfloat16)
        partial_sum = jnp.dot(attended.reshape(batch, local_heads * head_dim), w_out, preferred_element_type=jnp.float32) + jnp.dot(hidden, w_down, preferred_element_type=jnp.float32)
        summed = lax.psum(partial_sum, 'model')
        return (tokens.astype(jnp.float32) + summed).astype(jnp.bfloat16), key_new, value_new

    in_specs = (P('replica', None), P('replica'), P('replica', None, None, None), P('replica', None, None, None), P(None), P(None, 'model'), P(None, None), P(None, None), P('model', None), P(None, 'model'), P(None, 'model'), P('model', None))
    out_specs = (P('replica', None), P(('replica', 'model'), None, None), P(('replica', 'model'), None, None))
    return jax.shard_map(local_step, mesh=mesh, in_specs=in_specs, out_specs=out_specs, check_vma=False)
```

profile of v0, /device:TPU:0, one launch (start us, length us, event | category | flops | bytes accessed | tf_op | source)
XLA Modules:
  0.0 147.2 jit_solution(16526744970954301944)
XLA Ops:
  7.2 0.7 convert_element_type.54
  7.9 1.4 fusion.6
  9.3 0.7 convert_element_type.56
  9.9 1.4 fusion.8
  11.3 4.3 %fusion.49 = f32[128,768]{0,1:T(8,128)S(1)} fusion(bf16[128,3072]{1,0:T(8,128)(2,1)S(1)} %fusion.8, bf16[3072,768]{1,0:T(8,128)(2,1)} %param.17), kind=kOutput, calls=%fused_computation.63 | convolution fusion | flops 603979776 | bytes 5898240 | tf_op jit(solution)/shard_map/dot_general | solution.py:58
  15.9 0.9 copy.28
  16.8 4.6 %all-to-all-start = ((bf16[128,6,128]{2,1,0:T(8,128)(2,1)}), bf16[128,6,128]{2,1,0:T(8,128)(2,1)S(1)}, u32[]{:S(2)}, u32[]{:S(2)}) async-start(bf16[128,6,128]{2,1,0:T(8,128)(2,1)} %copy.28), calls=%async_computation | async-start | bytes 524288 | tf_op jit(solution)/shard_map/all_to_all | solution.py:59
  21.5 4.0 %convolution_bitcast_fusion = f32[4,8,8,128]{3,1,2,0:T(8,128)S(1)} fusion(bf16[3072,1024]{1,0:T(8,128)(2,1)} %param.18, bf16[128,3072]{1,0:T(8,128)(2,1)S(1)} %fusion.8, s32[]{:T(128)S(6)} %select_n.10), kind=kOutput, calls=%fused_computation.18 | convolution fusion | flops 201326592 | bytes 6619140 | tf_op jit(solution)/shard_map/dot_general | solution.py:62
  25.6 4.0 %fusion.13 = bf16[4,8,8,128]{3,1,2,0:T(8,128)(2,1)S(1)} fusion(bf16[3072,1024]{1,0:T(8,128)(2,1)} %param.19, bf16[128,3072]{1,0:T(8,128)(2,1)S(1)} %fusion.8, s32[]{:T(128)S(6)} %select_n.10), kind=kOutput, calls=%fused_computation.20 | convolution fusion | flops 201359360 | bytes 6553604 | tf_op jit(solution)/shard_map/dot_general | solution.py:63
  29.6 0.6 copy-done.1
  30.3 0.7 bitcast_convert_fusion
  30.9 10.1 %fusion.50 = f32[128,3072]{1,0:T(8,128)} fusion(bf16[128,3072]{1,0:T(8,128)(2,1)S(1)} %fusion.8, bf16[3072,3072]{1,0:T(8,128)(2,1)} %param.21), kind=kOutput, calls=%fused_computation.64 | convolution fusion | flops 2415919104 | bytes 21233664 | tf_op jit(solution)/shard_map/dot_general | solution.py:68
  41.4 0.4 fusion.32
  41.8 14.1 %fusion.5 = (f32[32,8,3]{2,1,0:T(8,128)S(1)}, f32[32,8,3,512]{3,2,1,0:T(4,128)S(1)}) fusion(pred[32,512]{1,0:T(8,128)(4,1)S(1)} %iota_compare_fusion, bf16[128,8,512,128]{3,2,1,0:T(8,128)(2,1)} %param.14, s32[]{:T(128)S(6)} %select_n.10, bf16[32,8,3,128]{3,0,2,1:T(8,128)(2,1)S(1)} %bitcast.38), kind=kOutput, calls=%fused_computation.12 | convolution fusion | flops 101842176 | bytes 35343364 | tf_op jit(solution)/shard_map/bgrd,bgtd->bgrt/dot_general | solution.py:34
  56.0 1.9 %fusion.14 = f32[32,8,3]{2,1,0:T(8,128)S(1)} fusion(f32[32,8,3,512]{3,2,1,0:T(4,128)S(1)} %get-tuple-element.16, f32[32,8,3]{2,1,0:T(8,128)S(1)} %multiply_maximum_fusion, pred[32,512]{1,0:T(8,128)(4,1)S(1)} %iota_compare_fusion), kind=kLoop, calls=%fused_computation.21 | loop fusion | flops 1572096 | bytes 1595392 | tf_op jit(solution)/shard_map/reduce_sum | solution.py:41
  57.9 0.7 convert_convert_fusion
  58.6 13.3 %fusion.26 = bf16[32,8,3,128]{3,2,1,0:T(4,128)(2,1)S(1)} fusion(bf16[128,8,512,128]{3,2,1,0:T(8,128)(2,1)} %param.15, s32[]{:T(128)S(6)} %select_n.10, f32[32,8,3,512]{3,2,1,0:T(4,128)S(1)} %get-tuple-element.16, f32[32,8,3]{2,1,0:T(8,128)S(1)} %multiply_maximum_fusion, pred[32,512]{1,0:T(8,128)(4,1)S(1)} %iota_compare_fusion, ...), kind=kOutput, calls=%fused_computation.28 | convolution fusion | flops 102629376 | bytes 35608580 | tf_op jit(solution)/shard_map/bgrt,bgtd->bgrd/dot_general | solution.py:42
  71.9 0.8 copy.32
  72.7 3.6 %all-to-all-start.1 = ((bf16[32,24,128]{2,0,1:T(8,128)(2,1)}), bf16[32,24,128]{2,0,1:T(8,128)(2,1)S(1)}, u32[]{:S(2)}, u32[]{:S(2)}) async-start(bf16[32,24,128]{2,0,1:T(8,128)(2,1)} %bitcast.8), calls=%async_computation.1 | async-start | bytes 393216 | tf_op jit(solution)/shard_map/all_to_all | solution.py:67
  76.3 17.5 %fusion.31 = f32[128,3072]{1,0:T(8,128)S(1)} fusion(bf16[3072,3072]{1,0:T(8,128)(2,1)} %param.23, bf16[128,3072]{1,0:T(8,128)(2,1)S(1)} %fusion.8, bf16[3072,3072]{1,0:T(8,128)(2,1)} %param.22, f32[128,3072]{1,0:T(8,128)} %fusion.50), kind=kOutput, calls=%fused_computation.29 | convolution fusion | flops 4834197504 | bytes 41680896 | tf_op jit(solution)/shard_map/dot_general | solution.py:69
  94.0 4.3 %convolution_add_fusion = f32[128,3072]{1,0:T(8,128)} fusion(f32[128,3072]{1,0:T(8,128)S(1)} %fusion.31, bf16[768,3072]{1,0:T(8,128)(2,1)} %param.20, bf16[16,8,6,128]{3,2,1,0:T(8,128)(2,1)S(1)} %bitcast.36), kind=kOutput, calls=%fused_computation.5 | convolution fusion | flops 604372992 | bytes 8060928 | tf_op jit(solution)/shard_map/dot_general | solution.py:69
  98.3 0.7 pad_maximum_fusion.1
  99.0 38.9 %all-reduce.2.cloned.1.call-done = f32[128,3072]{1,0:T(8,128)} async-done(((f32[128,3072]{1,0:T(8,128)}), f32[128,3072]{1,0:T(8,128)}) %all-reduce.2.cloned.1.call-update) | async-done | bytes 1572880 | tf_op jit(solution)/shard_map/psum | solution.py:70
  137.9 2.4 %fusion.9 = bf16[128,3072]{1,0:T(8,128)(2,1)} fusion(f32[128,3072]{1,0:T(8,128)} %all-reduce.2.cloned.1.call-done, bf16[128,3072]{1,0:T(8,128)(2,1)S(1)} %copy-done), kind=kLoop, calls=%fused_computation.16 | loop fusion | flops 1179648 | bytes 3145728 | tf_op jit(solution)/shard_map/convert_element_type | solution.py:71
  (24 shorter events, 1.0 us)
Async XLA Ops:
  15.6 5.8 %copy-start.2 = (s32[128]{0:T(128)S(1)}, s32[128]{0:T(128)}, u32[]{:S(2)}) copy-start(s32[128]{0:T(128)} %param.13) | copy-start | bytes 1540
  16.8 24.6 %all-to-all-start = ((bf16[128,6,128]{2,1,0:T(8,128)(2,1)}), bf16[128,6,128]{2,1,0:T(8,128)(2,1)S(1)}, u32[]{:S(2)}, u32[]{:S(2)}) async-start(bf16[128,6,128]{2,1,0:T(8,128)(2,1)} %copy.28), calls=%async_computation | async-start | bytes 524288 | tf_op jit(solution)/shard_map/all_to_all | solution.py:59
  29.6 0.6 copy-start.1
  72.7 21.2 %all-to-all-start.1 = ((bf16[32,24,128]{2,0,1:T(8,128)(2,1)}), bf16[32,24,128]{2,0,1:T(8,128)(2,1)S(1)}, u32[]{:S(2)}, u32[]{:S(2)}) async-start(bf16[32,24,128]{2,0,1:T(8,128)(2,1)} %bitcast.8), calls=%async_computation.1 | async-start | bytes 393216 | tf_op jit(solution)/shard_map/all_to_all | solution.py:67
  76.3 61.6 %all-reduce.2.cloned.1.call-start = ((), (), s32[]{:S(2)}) async-start(), calls=%async_computation.2 | async-start | bytes 3145728 | tf_op jit(solution)/shard_map/psum | solution.py:70
  98.3 39.6 %copy-start = (bf16[128,3072]{1,0:T(8,128)(2,1)S(1)}, bf16[128,3072]{1,0:T(8,128)(2,1)}, u32[]{:S(2)}) copy-start(bf16[128,3072]{1,0:T(8,128)(2,1)} %param.12) | copy-start | bytes 2359300
Sparse Core Ops, SparseCore 0:
  98.4 39.4 all-reduce.1
where the time goes:
time: 148 us; the launch traced here: 147 us
  matrix products  72 us (49%)
  waiting for transfers between devices  38.9 us (26%)
  between operations  14.2 us (10%)
  other arithmetic  11.4 us (8%)
  starting transfers between devices  8.24 us (6%)
  local copies, waits for them, and re-layouts  2.46 us (2%)
    psum x1, waiting for transfers between devices, local_step(): summed = lax.psum(partial_sum, 'model')  38.9 us
    dot_general x1, matrix products, local_step(): jnp.dot(hidden, w_down, preferred_element_type=jnp.float32)  17.5 us
    dot_general x1, matrix products, attend(): jnp.einsum('bgrd,bgtd->bgrt', grouped, key_rows, preferred_element_type=j...  14.1 us
    dot_general x1, matrix products, attend(): jnp.einsum('bgrt,bgtd->bgrd', weights.astype(jnp.bfloat16), value_rows, p...  13.3 us
    dot_general x1, matrix products, local_step(): jnp.dot(normed, w_gate, preferred_element_type=jnp.float32)  10.1 us
    all_to_all x1, starting transfers between devices, local_step(): queries = lax.all_to_all(queries, 'model', 0, 1, tiled=True)  4.61 us
    dot_general x1, matrix products, local_step(): jnp.dot(attended.reshape(batch, local_heads * head_dim), w_out, preferred...  4.28 us
    dot_general x1, matrix products, local_step(): jnp.dot(normed, w_query, preferred_element_type=jnp.float32)  4.28 us
  transfers between devices with their start and end apart: 3, of which 1 were waited for; matrix products, arithmetic and copies ran while one was open for 26% of the time, Pallas kernels for 0%

commit v1 on v0

v1 whole, which is shorter than its diff:
```python
import functools
import math

import jax
import jax.numpy as jnp
from jax import lax
from jax.experimental import pallas as pl
from jax.experimental.pallas import tpu as pltpu
from jax.sharding import PartitionSpec as P

ROPE_BASE = 10000.0
NORM_EPS = 1e-6
MASK_VALUE = -1e30
MESH = pl.DeviceIdType.MESH
F32 = jnp.float32
BF16 = jnp.bfloat16
TILE = 256
SLOTS = 8
AHEAD = SLOTS // 2


def rms_norm(tokens, norm_gain):
    values = tokens.astype(F32)
    mean_sq = jnp.mean(values * values, axis=-1, keepdims=True)
    return (values * lax.rsqrt(mean_sq + NORM_EPS) * norm_gain.astype(F32)).astype(BF16)


def apply_rope(values, positions):
    half_dim = values.shape[-1] // 2
    inv_freq = jnp.exp(jnp.arange(half_dim, dtype=F32) * (-2.0 * math.log(ROPE_BASE) / values.shape[-1]))
    angles = positions.astype(F32)[:, None, None] * inv_freq[None, None, :]
    cos_part = jnp.cos(angles)
    sin_part = jnp.sin(angles)
    first_half = values[..., :half_dim]
    second_half = values[..., half_dim:]
    return jnp.concatenate([first_half * cos_part - second_half * sin_part, second_half * cos_part + first_half * sin_part], axis=-1)


def attend(queries, key_rows, value_rows, key_new, value_new, row_lengths):
    row_count, heads, head_dim = queries.shape
    kv_heads = key_rows.shape[1]
    grouped = queries.reshape(row_count, kv_heads, heads // kv_heads, head_dim)
    scale = head_dim ** -0.5
    scores = jnp.einsum('bgrd,bgtd->bgrt', grouped, key_rows, preferred_element_type=F32) * scale
    valid = jnp.arange(key_rows.shape[2])[None, None, None, :] < row_lengths[:, None, None, None]
    scores = jnp.where(valid, scores, MASK_VALUE)
    score_new = jnp.einsum('bgrd,bgd->bgr', grouped, key_new, preferred_element_type=F32) * scale
    peak = jnp.maximum(jnp.max(scores, axis=-1), score_new)
    weights = jnp.exp(scores - peak[..., None])
    weight_new = jnp.exp(score_new - peak)
    total = jnp.sum(weights, axis=-1) + weight_new
    mixed = jnp.einsum('bgrt,bgtd->bgrd', weights.astype(BF16), value_rows, preferred_element_type=F32)
    mixed = mixed + weight_new.astype(BF16).astype(F32)[..., None] * value_new.astype(F32)[:, :, None, :]
    return (mixed / total[..., None]).astype(BF16).reshape(row_count, heads * head_dim)


def mlp_kernel(normed, tokens, attended, kv_new, w_gate, w_up, w_down, w_out,
               y_out, key_out, value_out,
               h_buf, x_buf, o_buf, kv_buf, w_buf, wo_buf, u_buf, part, from_sib, to_cross, from_cross, y_buf, kv_in, head_buf,
               in_sem, w_sem, wo_sem, kv_send, kv_recv, s1_send, s1_recv, s2_send, s2_recv,
               yc_send, yc_recv, ys_send, ys_recv, yr_send, yr_recv, out_sem):
    me = lax.axis_index('model')
    core = lax.rem(me, 2)
    chip = lax.div(me, 2)
    sib = chip * 2 + (1 - core)
    cross = (1 - chip) * 2 + core
    diag = (1 - chip) * 2 + (1 - core)
    model_dim = w_gate.shape[0]
    width = w_gate.shape[1]
    n_hid = width // TILE
    n_out = model_dim // TILE
    head_dim = head_buf.shape[2]
    local_kv = kv_new.shape[2] // (2 * head_dim)

    barrier = pltpu.get_barrier_semaphore()
    for peer in (sib, cross, diag):
        pl.semaphore_signal(barrier, inc=1, device_id={'model': peer}, device_id_type=MESH)

    def cols(tile):
        return pl.ds(pl.multiple_of(tile * TILE, TILE), TILE)

    def fetch(src, tile, slot):
        return pltpu.make_async_copy(src.at[:, cols(tile)], w_buf.at[slot], w_sem.at[slot])

    def remote(src, dst, send, recv, peer):
        return pltpu.make_async_remote_copy(src_ref=src, dst_ref=dst, send_sem=send, recv_sem=recv,
                                            device_id={'model': peer}, device_id_type=MESH)

    h_copy = pltpu.make_async_copy(normed, h_buf, in_sem.at[0])
    h_copy.start()
    for pair in range(AHEAD):
        fetch(w_gate, pair, 2 * pair).start()
        fetch(w_up, pair, 2 * pair + 1).start()
    x_copy = pltpu.make_async_copy(tokens.at[me], x_buf, in_sem.at[1])
    o_copy = pltpu.make_async_copy(attended, o_buf, in_sem.at[2])
    kv_copy = pltpu.make_async_copy(kv_new, kv_buf, in_sem.at[3])
    for copy in (x_copy, o_copy, kv_copy):
        copy.start()
    h_copy.wait()

    def hidden_tile(j):
        slot = lax.rem(2 * j, SLOTS)
        fetch(w_gate, j, slot).wait()
        gate = jnp.dot(h_buf[...], w_buf[slot], preferred_element_type=F32)
        fetch(w_up, j, slot + 1).wait()
        up = jnp.dot(h_buf[...], w_buf[slot + 1], preferred_element_type=F32)
        u_buf[:, cols(j)] = (jax.nn.silu(gate) * up).astype(BF16)
        return slot

    @pl.loop(0, n_hid - AHEAD)
    def _(j):
        slot = hidden_tile(j)
        fetch(w_gate, j + AHEAD, slot).start()
        fetch(w_up, j + AHEAD, slot + 1).start()

    wo_copy = pltpu.make_async_copy(w_out, wo_buf, wo_sem)
    wo_copy.start()
    kv_copy.wait()
    pl.semaphore_wait(barrier, 3)
    kv_sends = []
    for n, peer in enumerate((sib, cross, diag)):
        send = remote(kv_buf.at[peer], kv_in.at[me], kv_send.at[n], kv_recv.at[n], peer)
        send.start()
        kv_sends.append(send)

    @pl.loop(n_hid - AHEAD, n_hid)
    def _(j):
        slot = hidden_tile(j)
        tile = 2 * (j - (n_hid - AHEAD))
        fetch(w_down, tile, slot).start()
        fetch(w_down, tile + 1, slot + 1).start()

    x_copy.wait()
    o_copy.wait()
    wo_copy.wait()

    def sib_send(c):
        return remote(part.at[c, :, 1 - core], from_sib.at[c], s1_send.at[c], s1_recv.at[c], sib)

    def cross_send(c):
        return remote(to_cross.at[c], from_cross.at[c], s2_send.at[c], s2_recv.at[c], cross)

    def y_cross(c):
        return remote(y_buf.at[c, me], y_buf.at[c, me], yc_send.at[c], yc_recv.at[c], cross)

    def y_sib(c):
        return remote(y_buf.at[c, me], y_buf.at[c, me], ys_send.at[c], ys_recv.at[c], sib)

    def y_relay(c):
        return remote(y_buf.at[c, cross], y_buf.at[c, cross], yr_send.at[c], yr_recv.at[c], sib)

    def y_store(c):
        return pltpu.make_async_copy(y_buf.at[c], y_out.at[:, :, cols(c)], out_sem.at[c])

    @pl.loop(0, n_out + 6)
    def _(i):
        @pl.when(i < n_out)
        def _():
            slot = lax.rem(i, SLOTS)
            fetch(w_down, i, slot).wait()
            total = jnp.dot(u_buf[...], w_buf[slot], preferred_element_type=F32)
            total += jnp.dot(o_buf[...], wo_buf[:, cols(i)], preferred_element_type=F32)
            part[i] = total.reshape(part.shape[1:])
            sib_send(i).start()

        @pl.when(i < n_out - SLOTS)
        def _():
            fetch(w_down, i + SLOTS, lax.rem(i, SLOTS)).start()

        @pl.when((i >= 1) & (i < n_out + 1))
        def _():
            c = i - 1
            sib_send(c).wait_recv()
            to_cross[c] = part[c, 1 - chip, core] + from_sib[c, 1 - chip]
            cross_send(c).start()

        @pl.when((i >= 3) & (i < n_out + 3))
        def _():
            c = i - 3
            cross_send(c).wait_recv()
            total = part[c, chip, core] + from_sib[c, chip] + from_cross[c]
            y_buf[c, me] = (x_buf[:, cols(c)].astype(F32) + total).astype(BF16)
            y_cross(c).start()
            y_sib(c).start()

        @pl.when((i >= 5) & (i < n_out + 5))
        def _():
            c = i - 5
            y_cross(c).wait_recv()
            y_relay(c).start()

        @pl.when(i == n_out)
        def _():
            for send in kv_sends:
                send.wait_recv()
            kv_in[me] = kv_buf[me]
            for half, out in enumerate((key_out, value_out)):
                for source in range(kv_in.shape[0]):
                    for g in range(local_kv):
                        start = (half * local_kv + g) * head_dim
                        head_buf[:, source * local_kv + g, :] = kv_in[source, :, start:start + head_dim].astype(F32)
                out[...] = head_buf[...].astype(BF16)

        @pl.when(i >= 6)
        def _():
            c = i - 6
            y_sib(c).wait_recv()
            y_relay(c).wait_recv()
            y_store(c).start()

    for send in kv_sends:
        send.wait_send()

    @pl.loop(0, n_out)
    def _(c):
        sib_send(c).wait_send()
        cross_send(c).wait_send()
        y_cross(c).wait_send()
        y_sib(c).wait_send()
        y_relay(c).wait_send()
        y_store(c).wait()


def mlp_and_sum(normed, tokens, attended, kv_new, w_gate, w_up, w_down, w_out, kv_heads, head_dim):
    batch, model_dim = normed.shape
    width = w_gate.shape[1]
    q_dim = w_out.shape[0]
    devices = 4
    rows = batch // devices
    n_out = model_dim // TILE
    kv_width = kv_new.shape[1]
    dma = pltpu.SemaphoreType.DMA
    hbm = pl.BlockSpec(memory_space=pl.ANY)
    vmem = pl.BlockSpec(memory_space=pltpu.VMEM)
    y, key_out, value_out = pl.pallas_call(
        mlp_kernel,
        out_shape=(jax.ShapeDtypeStruct((devices, rows, model_dim), BF16),
                   jax.ShapeDtypeStruct((rows, kv_heads, head_dim), BF16),
                   jax.ShapeDtypeStruct((rows, kv_heads, head_dim), BF16)),
        in_specs=[hbm] * 8,
        out_specs=(hbm, vmem, vmem),
        scratch_shapes=[
            pltpu.VMEM((batch, model_dim), BF16),
            pltpu.VMEM((rows, model_dim), BF16),
            pltpu.VMEM((batch, q_dim), BF16),
            pltpu.VMEM((devices, rows, kv_width), BF16),
            pltpu.VMEM((SLOTS, model_dim, TILE), BF16),
            pltpu.VMEM((q_dim, model_dim), BF16),
            pltpu.VMEM((batch, width), BF16),
            pltpu.VMEM((n_out, 2, 2, rows, TILE), F32),
            pltpu.VMEM((n_out, 2, rows, TILE), F32),
            pltpu.VMEM((n_out, rows, TILE), F32),
            pltpu.VMEM((n_out, rows, TILE), F32),
            pltpu.VMEM((n_out, devices, rows, TILE), BF16),
            pltpu.VMEM((devices, rows, kv_width), BF16),
            pltpu.VMEM((rows, kv_heads, head_dim), F32),
            dma((4,)), dma((SLOTS,)), dma, dma((3,)), dma((3,)),
        ] + [dma((n_out,))] * 11,
        compiler_params=pltpu.CompilerParams(collective_id=0, has_side_effects=True, vmem_limit_bytes=48 * 2 ** 20),
        name="mlp_and_sum",
    )(normed, tokens.reshape(devices, rows, model_dim), attended, kv_new.reshape(devices, rows, kv_width), w_gate, w_up, w_down, w_out)
    return y.reshape(batch, model_dim), key_out, value_out


def solution(mesh):
    groups = mesh.shape['model']

    def local_step(tokens, lengths, k_cache, v_cache, norm_gain, w_query, w_key, w_value, w_out, w_gate, w_up, w_down):
        batch = tokens.shape[0]
        kv_heads = k_cache.shape[1]
        head_dim = k_cache.shape[3]
        local_heads = w_query.shape[1] // head_dim
        local_kv = kv_heads // groups
        me = lax.axis_index('model')
        normed = rms_norm(tokens, norm_gain)
        queries = apply_rope(jnp.dot(normed, w_query, preferred_element_type=F32).reshape(batch, local_heads, head_dim), lengths).astype(BF16)
        wk = lax.dynamic_slice_in_dim(w_key, me * local_kv * head_dim, local_kv * head_dim, 1)
        wv = lax.dynamic_slice_in_dim(w_value, me * local_kv * head_dim, local_kv * head_dim, 1)
        key_new = apply_rope(jnp.dot(normed, wk, preferred_element_type=F32).reshape(batch, local_kv, head_dim), lengths).astype(BF16)
        value_new = jnp.dot(normed, wv, preferred_element_type=F32).reshape(batch, local_kv, head_dim).astype(BF16)
        key_rows = lax.dynamic_slice_in_dim(k_cache, me * local_kv, local_kv, 1)
        value_rows = lax.dynamic_slice_in_dim(v_cache, me * local_kv, local_kv, 1)
        attended = attend(queries, key_rows, value_rows, key_new, value_new, lengths)
        kv_new = jnp.concatenate([key_new.reshape(batch, -1), value_new.reshape(batch, -1)], axis=1)
        return mlp_and_sum(normed, tokens, attended, kv_new, w_gate, w_up, w_down, w_out, kv_heads, head_dim)

    in_specs = (P('replica', None), P('replica'), P('replica', None, None, None), P('replica', None, None, None), P(None), P(None, 'model'), P(None, None), P(None, None), P('model', None), P(None, 'model'), P(None, 'model'), P('model', None))
    out_specs = (P('replica', None), P(('replica', 'model'), None, None), P(('replica', 'model'), None, None))
    return jax.shard_map(local_step, mesh=mesh, in_specs=in_specs, out_specs=out_specs, check_vma=False)
```

time: 148 us -> 89.4 us (0.60)
  Pallas kernels: 0 us -> 39.8 us
  waiting for transfers between devices: 38.9 us -> 0 us
  matrix products: 72 us -> 37.3 us
  between operations: 14.2 us -> 0.87 us
  starting transfers between devices: 8.24 us -> 0 us
  other arithmetic: 11.4 us -> 6.64 us
  local copies, waits for them, and re-layouts: 2.46 us -> 4.5 us
    pallas_call x0 -> x1, Pallas kernels: none -> 39.8 us  [mlp_and_sum(): pl.pallas_call(mlp_kernel, out_shape=(jax.ShapeDtypeStruct((devices, rows...]
    psum x1 -> x0, waiting for transfers between devices: 38.9 us -> none  [local_step(): summed = lax.psum(partial_sum, 'model')]
    dot_general x9 -> x6, matrix products: 72 us -> 37.3 us  [the longest x1 14.9 us: attend(): jnp.einsum('bgrd,bgtd->bgrt', grouped, key_rows, preferred_element_type=F32)]
    all_to_all x2 -> x0, starting transfers between devices: 8.21 us -> none  [the longest x1 4.61 us: local_step(): queries = lax.all_to_all(queries, 'model', 0, 1, tiled=True)]
    convert_element_type x7 -> x6, other arithmetic: 6.63 us -> 2.63 us  [the longest x1 1.4 us: rms_norm(): (values * lax.rsqrt(mean_sq + NORM_EPS) * norm_gain.astype(F32)).astype(B...]
    unnamed x8 -> x9, local copies, waits for them, and re-layouts: 0.68 us -> 3.39 us
  transfers between devices with their start and end apart: 3 -> 0, of which waited for: 1 -> 0; matrix products, arithmetic and copies ran while one was open for 26% -> 0% of each run, Pallas kernels for 0% -> 0%
where the time goes in v1:
time: 89.4 us; the launch traced here: 89.1 us
  Pallas kernels  39.8 us (45%)
  matrix products  37.3 us (42%)
  other arithmetic  6.64 us (7%)
  local copies, waits for them, and re-layouts  4.5 us (5%)
    pallas_call x1, Pallas kernels, mlp_and_sum(): pl.pallas_call(mlp_kernel, out_shape=(jax.ShapeDtypeStruct((devices, rows...  39.8 us
    dot_general x1, matrix products, attend(): jnp.einsum('bgrd,bgtd->bgrt', grouped, key_rows, preferred_element_type=F32)  14.9 us
    dot_general x1, matrix products, attend(): jnp.einsum('bgrt,bgtd->bgrd', weights.astype(BF16), value_rows, preferred...  14 us
    dot_general x1, matrix products, local_step(): jnp.dot(normed, w_query, preferred_element_type=F32)  4.28 us
    unnamed x9, local copies, waits for them, and re-layouts  3.39 us
    reduce_sum x1, other arithmetic, attend(): total = jnp.sum(weights, axis=-1) + weight_new  1.86 us
    dot_general x1, matrix products, local_step(): jnp.dot(normed, wv, preferred_element_type=F32)  1.79 us
    dot_general x1, matrix products, local_step(): jnp.dot(normed, wk, preferred_element_type=F32)  1.79 us

profile of v1, /device:TPU:0, one launch (start us, length us, event | category | flops | bytes accessed | tf_op | source)
XLA Modules:
  0.0 89.1 jit_solution(6377273953664599161)
XLA Ops:
  0.6 0.7 convert_element_type.55
  1.3 1.4 %fusion.5 = f32[128]{0:T(128)S(1)} fusion(bf16[128,3072]{1,0:T(8,128)(2,1)} %param.12), kind=kLoop, calls=%fused_computation.9 | loop fusion | flops 1179520 | bytes 786944 | tf_op jit(solution)/shard_map/reduce_sum | solution.py:24
  2.7 1.4 %fusion.7.normed = bf16[128,3072]{1,0:T(8,128)(2,1)S(1)} fusion(bf16[128,3072]{1,0:T(8,128)(2,1)} %param.12, f32[3072]{0:T(1024)S(1)} %convert_element_type.55, f32[128]{0:T(128)S(1)} %add_rsqrt_fusion), kind=kLoop, calls=%fused_computation.11 | loop fusion | flops 1572864 | bytes 1585664 | tf_op jit(solution)/shard_map/convert_element_type | solution.py:25
  4.1 1.8 %fusion.10 = f32[128,256]{1,0:T(8,128)S(1)} fusion(bf16[128,3072]{1,0:T(8,128)(2,1)S(1)} %fusion.7.normed, bf16[3072,1024]{1,0:T(8,128)(2,1)} %param.18, s32[]{:T(128)S(6)} %select_n.14), kind=kOutput, calls=%fused_computation.14 | convolution fusion | flops 201326592 | bytes 2490372 | tf_op jit(solution)/shard_map/dot_general | solution.py:279
  6.0 0.2 multiply_cosine_fusion
  6.4 0.3 multiply_subtract_fusion
  6.7 0.2 fusion.49
  6.9 4.3 %fusion.44 = f32[128,768]{0,1:T(8,128)S(1)} fusion(bf16[128,3072]{1,0:T(8,128)(2,1)S(1)} %fusion.7.normed, bf16[3072,768]{1,0:T(8,128)(2,1)} %param.17), kind=kOutput, calls=%fused_computation.50 | convolution fusion | flops 603979776 | bytes 5898240 | tf_op jit(solution)/shard_map/dot_general | solution.py:276
  11.3 0.2 copy.16
  11.5 0.2 copy.17
  11.7 0.5 fusion.35
  12.3 14.9 %fusion.4 = (f32[128,2,3]{2,1,0:T(2,128)S(1)}, f32[128,2,3,512]{3,2,1,0:T(4,128)S(1)}) fusion(pred[128,512]{1,0:T(8,128)(4,1)S(1)} %iota_compare_fusion, bf16[128,8,512,128]{3,2,1,0:T(8,128)(2,1)} %param.14, s32[]{:T(128)S(6)} %select_n.12, bf16[128,2,3,64]{3,2,1,0:T(4,128)(2,1)S(1)} %copy.17, bf16[128,2,3,64]{3,2,1,0:T(4,128)(2,1)S(1)} %copy.16), kind=kOutput, calls=%fused_computation.8 | convolution fusion | flops 102235392 | bytes 35392516 | tf_op jit(solution)/shard_map/bgrd,bgtd->bgrt/dot_general | solution.py:44
  27.4 1.2 %copy-done.1 = f32[128,2,3,512]{3,2,1,0:T(4,128)} copy-done((f32[128,2,3,512]{3,2,1,0:T(4,128)}, f32[128,2,3,512]{3,2,1,0:T(4,128)S(1)}, u32[]{:S(2)}) %copy-start.1) | copy-done | bytes 1572888
  28.6 1.9 %fusion.18 = f32[128,2,3]{2,1,0:T(2,128)S(1)} fusion(f32[128,2,3,512]{3,2,1,0:T(4,128)S(1)} %get-tuple-element.18, f32[128,2,3]{2,1,0:T(2,128)S(1)} %multiply_maximum_fusion, pred[128,512]{1,0:T(8,128)(4,1)S(1)} %iota_compare_fusion), kind=kLoop, calls=%fused_computation.18 | loop fusion | flops 1572096 | bytes 1644544 | tf_op jit(solution)/shard_map/reduce_sum | solution.py:51
  30.5 0.2 convert_convert_fusion
  30.6 1.8 %fusion.15 = bf16[128,256]{1,0:T(8,128)(2,1)S(1)} fusion(bf16[128,3072]{1,0:T(8,128)(2,1)S(1)} %fusion.7.normed, bf16[3072,1024]{1,0:T(8,128)(2,1)} %param.19, s32[]{:T(128)S(6)} %select_n.14), kind=kOutput, calls=%fused_computation.17 | convolution fusion | flops 201359360 | bytes 2424836 | tf_op jit(solution)/shard_map/dot_general | solution.py:280
  32.5 14.0 %fusion.30 = bf16[128,2,3,128]{3,2,1,0:T(4,128)(2,1)S(1)} fusion(bf16[128,8,512,128]{3,2,1,0:T(8,128)(2,1)} %param.15, s32[]{:T(128)S(6)} %select_n.12, f32[128,2,3,512]{3,2,1,0:T(4,128)} %copy-done.1, f32[128,2,3]{2,1,0:T(2,128)S(1)} %multiply_maximum_fusion, pred[128,512]{1,0:T(8,128)(4,1)S(1)} %iota_compare_fusion, ...), kind=kOutput, calls=%fused_computation.25 | convolution fusion | flops 102629376 | bytes 36054020 | tf_op jit(solution)/shard_map/bgrt,bgtd->bgrd/dot_general | solution.py:52
  46.5 0.2 copy.20
  46.7 0.2 copy.21.attended
  46.9 0.2 maximum_convert_fusion
  47.1 39.8 %mlp_and_sum.1 = (bf16[4,32,3072]{2,1,0:T(8,128)(2,1)S(1)}, bf16[32,8,128]{2,1,0:T(8,128)(2,1)S(1)}, bf16[32,8,128]{2,1,0:T(8,128)(2,1)S(1)}) custom-call(bf16[128,3072]{1,0:T(8,128)(2,1)S(1)} %fusion.7.normed, bf16[4,32,3072]{2,1,0:T(8,128)(2,1)S(1)} %bitcast.15, bf16[128,768]{1,0:T(8,128)(2,1)S(1)} %copy.21.attended, ...), custom_call_target="tpu_custom_call" | custom-call | tf_op jit(solution)/shard_map/mlp_and_sum/pallas_call | solution.py:235
  86.9 0.9 copy.30
  87.8 0.6 copy.31
  88.4 0.6 copy.32
  (17 shorter events, 0.7 us)
Async XLA Ops:
  2.7 3.3 %copy-start.2 = (s32[128]{0:T(128)S(1)}, s32[128]{0:T(128)}, u32[]{:S(2)}) copy-start(s32[128]{0:T(128)} %param.13) | copy-start | bytes 1540
  27.2 1.3 %copy-start.1 = (f32[128,2,3,512]{3,2,1,0:T(4,128)}, f32[128,2,3,512]{3,2,1,0:T(4,128)S(1)}, u32[]{:S(2)}) copy-start(f32[128,2,3,512]{3,2,1,0:T(4,128)S(1)} %get-tuple-element.18) | copy-start | bytes 4718596
  32.5 14.6 %copy-start = (bf16[128,3072]{1,0:T(8,128)(2,1)S(1)}, bf16[128,3072]{1,0:T(8,128)(2,1)}, u32[]{:S(2)}) copy-start(bf16[128,3072]{1,0:T(8,128)(2,1)} %param.12) | copy-start | bytes 2359300

commit v2 on v1

--- a/solution.py
+++ b/solution.py
@@ -19,46 +19,219 @@
 AHEAD = SLOTS // 2
 
 
-def rms_norm(tokens, norm_gain):
-    values = tokens.astype(F32)
-    mean_sq = jnp.mean(values * values, axis=-1, keepdims=True)
-    return (values * lax.rsqrt(mean_sq + NORM_EPS) * norm_gain.astype(F32)).astype(BF16)
-
-
-def apply_rope(values, positions):
-    half_dim = values.shape[-1] // 2
-    inv_freq = jnp.exp(jnp.arange(half_dim, dtype=F32) * (-2.0 * math.log(ROPE_BASE) / values.shape[-1]))
-    angles = positions.astype(F32)[:, None, None] * inv_freq[None, None, :]
+CHUNK = 64
+GROUP = 32
+UNROLL = 8
+
+
+def rope_tables(positions, head_dim):
+    half_dim = head_dim // 2
+    inv_freq = jnp.exp(jnp.arange(half_dim, dtype=F32) * (-2.0 * math.log(ROPE_BASE) / head_dim))
+    angles = positions.astype(F32)[:, None] * inv_freq[None, :]
     cos_part = jnp.cos(angles)
     sin_part = jnp.sin(angles)
-    first_half = values[..., :half_dim]
-    second_half = values[..., half_dim:]
-    return jnp.concatenate([first_half * cos_part - second_half * sin_part, second_half * cos_part + first_half * sin_part], axis=-1)
-
-
-def attend(queries, key_rows, value_rows, key_new, value_new, row_lengths):
-    row_count, heads, head_dim = queries.shape
-    kv_heads = key_rows.shape[1]
-    grouped = queries.reshape(row_count, kv_heads, heads // kv_heads, head_dim)
+    return jnp.concatenate([cos_part, cos_part], axis=-1), jnp.concatenate([-sin_part, sin_part], axis=-1)
+
+
+def attend_kernel(lengths, tokens, gain, cos_part, sin_part, k_cache, v_cache, w_query, w_key, w_value,
+                  h_out, o_out, kv_out,
+                  x_buf, w_buf, k_buf, v_buf, q_buf, kn_buf, vn_buf, score, peak, total, mixed,
+                  item_row, item_pos, count, x_sem, w_sem, k_sem, v_sem):
+    batch, model_dim = tokens.shape
+    head_dim = cos_part.shape[1]
+    local_kv = kv_out.shape[1] // (2 * head_dim)
+    heads = o_out.shape[1] // head_dim
+    ratio = heads // local_kv
+    q_tiles = w_query.shape[1] // TILE
+    per_tile = TILE // head_dim
+    n_groups = batch // GROUP
     scale = head_dim ** -0.5
-    scores = jnp.einsum('bgrd,bgtd->bgrt', grouped, key_rows, preferred_element_type=F32) * scale
-    valid = jnp.arange(key_rows.shape[2])[None, None, None, :] < row_lengths[:, None, None, None]
-    scores = jnp.where(valid, scores, MASK_VALUE)
-    score_new = jnp.einsum('bgrd,bgd->bgr', grouped, key_new, preferred_element_type=F32) * scale
-    peak = jnp.maximum(jnp.max(scores, axis=-1), score_new)
-    weights = jnp.exp(scores - peak[..., None])
-    weight_new = jnp.exp(score_new - peak)
-    total = jnp.sum(weights, axis=-1) + weight_new
-    mixed = jnp.einsum('bgrt,bgtd->bgrd', weights.astype(BF16), value_rows, preferred_element_type=F32)
-    mixed = mixed + weight_new.astype(BF16).astype(F32)[..., None] * value_new.astype(F32)[:, :, None, :]
-    return (mixed / total[..., None]).astype(BF16).reshape(row_count, heads * head_dim)
-
-
-def mlp_kernel(normed, tokens, attended, kv_new, w_gate, w_up, w_down, w_out,
+    me = lax.axis_index('model')
+    first_kv = me * local_kv
+
+    x_copy = pltpu.make_async_copy(tokens, x_buf, x_sem)
+    x_copy.start()
+    kv_cols = pl.ds(pl.multiple_of(me * TILE, TILE), TILE)
+    w_copies = [pltpu.make_async_copy(w_query.at[:, t * TILE:(t + 1) * TILE], w_buf.at[t], w_sem.at[t]) for t in range(q_tiles)]
+    w_copies.append(pltpu.make_async_copy(w_key.at[:, kv_cols], w_buf.at[q_tiles], w_sem.at[q_tiles]))
+    w_copies.append(pltpu.make_async_copy(w_value.at[:, kv_cols], w_buf.at[q_tiles + 1], w_sem.at[q_tiles + 1]))
+    for copy in w_copies:
+        copy.start()
+
+    def fetch(cache, buf, sem, seq, row, pos, par):
+        return pltpu.make_async_copy(cache.at[seq, pl.ds(first_kv, local_kv), pl.ds(pl.multiple_of(pos, CHUNK), CHUNK)],
+                                     buf.at[par, row, :, pl.ds(pl.multiple_of(pos, CHUNK), CHUNK)], sem.at[par])
+
+    def issue(g):
+        par = g % 2
+
+        def one_seq(row, k):
+            seq = g * GROUP + row
+
+            def one_chunk(c, k):
+                pos = c * CHUNK
+                fetch(k_cache, k_buf, k_sem, seq, row, pos, par).start()
+                fetch(v_cache, v_buf, v_sem, seq, row, pos, par).start()
+                item_row[par, k] = row
+                item_pos[par, k] = pos
+                return k + 1
+
+            return lax.fori_loop(0, lax.div(lengths[seq] + (CHUNK - 1), CHUNK), one_chunk, k)
+
+        n = lax.fori_loop(0, GROUP, one_seq, 0)
+        for u in range(UNROLL - 1):
+            item_row[par, n + u] = GROUP
+            item_pos[par, n + u] = 0
+        count[par] = n
+
+    issue(0)
+    issue(1)
+
+    x_copy.wait()
+    x = x_buf[...].astype(F32)
+    mean_sq = jnp.mean(x * x, axis=-1, keepdims=True)
+    h_out[...] = (x * lax.rsqrt(mean_sq + NORM_EPS) * gain[...].astype(F32)).astype(BF16)
+
+    def rope(a):
+        return a * cos_part[...] + pltpu.roll(a, head_dim // 2, 1) * sin_part[...]
+
+    for t, copy in enumerate(w_copies):
+        copy.wait()
+        prod = jnp.dot(h_out[...], w_buf[t], preferred_element_type=F32)
+        for j in range(per_tile):
+            a = prod[:, j * head_dim:(j + 1) * head_dim]
+            if t < q_tiles:
+                q_buf[:, t * per_tile + j, :] = rope(a).astype(BF16).astype(F32)
+            else:
+                a = (rope(a) if t == q_tiles else a).astype(BF16)
+                col = ((t - q_tiles) * local_kv + j) * head_dim
+                kv_out[:, col:col + head_dim] = a
+                for r in range(ratio):
+                    (kn_buf if t == q_tiles else vn_buf)[:, j * ratio + r, :] = a.astype(F32)
+    for h in range(heads, q_buf.shape[1]):
+        zero = jnp.zeros((batch, head_dim), F32)
+        q_buf[:, h, :] = zero
+        kn_buf[:, h, :] = zero
+        vn_buf[:, h, :] = zero
+
+    sub = q_buf.shape[1]
+    lane = lax.broadcasted_iota(jnp.int32, (sub, local_kv * CHUNK), 1)
+    head = lax.broadcasted_iota(jnp.int32, (sub, local_kv * CHUNK), 0)
+    own = (lax.div(lane, CHUNK) == lax.div(head, ratio)) & (head < heads)
+    pos_in = jnp.where(own, lax.rem(lane, CHUNK), 1 << 20)
+
+    for g in range(n_groups):
+        par = g % 2
+        base = g * GROUP
+        n = count[par]
+        steps = lax.div(n + (UNROLL - 1), UNROLL)
+
+        def wait_all(cache, buf, sem):
+            @pl.loop(0, n)
+            def _(k):
+                fetch(cache, buf, sem, 0, 0, 0, par).wait()
+
+        peak[...] = jnp.full(peak.shape, MASK_VALUE, F32)
+        total[...] = jnp.zeros(total.shape, F32)
+        mixed[...] = jnp.zeros(mixed.shape, F32)
+        wait_all(k_cache, k_buf, k_sem)
+
+        def slot(k):
+            row = item_row[par, k]
+            pos = item_pos[par, k]
+            return row, jnp.minimum(row, GROUP - 1), pos
+
+        @pl.loop(0, steps)
+        def _(step):
+            found = []
+            for u in range(UNROLL):
+                k = step * UNROLL + u
+                row, at, pos = slot(k)
+                keys = k_buf[par, at, :, pl.ds(pl.multiple_of(pos, CHUNK), CHUNK), :].reshape(local_kv * CHUNK, head_dim)
+                s = lax.dot_general(q_buf[base + at].astype(BF16), keys, (((1,), (1,)), ((), ())), preferred_element_type=F32) * scale
+                s = jnp.where(pos_in < jnp.where(row < GROUP, lengths[base + at], 0) - pos, s, MASK_VALUE)
+                score[k] = s
+                found.append((row, s))
+            for row, s in found:
+                peak[row] = jnp.maximum(peak[row], s)
+
+        q = q_buf[base:base + GROUP]
+        score_new = jnp.sum(q * kn_buf[base:base + GROUP], axis=-1, keepdims=True) * scale
+        top = jnp.maximum(jnp.max(peak[:GROUP], axis=-1, keepdims=True), score_new)
+        weight_new = jnp.exp(score_new - top)
+        peak[:GROUP] = jnp.broadcast_to(top, (GROUP, sub, peak.shape[2]))
+
+        wait_all(v_cache, v_buf, v_sem)
+
+        @pl.loop(0, steps)
+        def _(step):
+            found = []
+            for u in range(UNROLL):
+                k = step * UNROLL + u
+                row, at, pos = slot(k)
+                p = jnp.exp(score[k] - peak[at])
+                values = v_buf[par, at, :, pl.ds(pl.multiple_of(pos, CHUNK), CHUNK), :].reshape(local_kv * CHUNK, head_dim)
+                found.append((row, p, jnp.dot(p.astype(BF16), values, preferred_element_type=F32)))
+            for row, p, o in found:
+                total[row] = total[row] + p
+                mixed[row] = mixed[row] + o
+
+        if g + 2 < n_groups:
+            issue(g + 2)
+        norm = jnp.sum(total[:GROUP], axis=-1, keepdims=True) + weight_new
+        out = mixed[:GROUP] + weight_new.astype(BF16).astype(F32) * vn_buf[base:base + GROUP]
+        q_buf[base:base + GROUP] = out / norm
+
+    for h in range(heads):
+        o_out[:, h * head_dim:(h + 1) * head_dim] = q_buf[:, h, :].astype(BF16)
+
+
+def qkv_and_attend(tokens, lengths, k_cache, v_cache, norm_gain, w_query, w_key, w_value, groups):
+    batch, model_dim = tokens.shape
+    kv_heads, context, head_dim = k_cache.shape[1:]
+    local_kv = kv_heads // groups
+    q_dim = w_query.shape[1]
+    cos_part, sin_part = rope_tables(lengths, head_dim)
+    items = GROUP * (context // CHUNK) + UNROLL
+    lanes = local_kv * CHUNK
+    dma = pltpu.SemaphoreType.DMA
+    hbm = pl.BlockSpec(memory_space=pl.ANY)
+    vmem = pl.BlockSpec(memory_space=pltpu.VMEM)
+    smem = pl.BlockSpec(memory_space=pltpu.SMEM)
+    return pl.pallas_call(
+        attend_kernel,
+        out_shape=(jax.ShapeDtypeStruct((batch, model_dim), BF16),
+                   jax.ShapeDtypeStruct((batch, q_dim), BF16),
+                   jax.ShapeDtypeStruct((batch, 2 * local_kv * head_dim), BF16)),
+        in_specs=[smem, hbm, vmem, vmem, vmem, hbm, hbm, hbm, hbm, hbm],
+        out_specs=(vmem, vmem, vmem),
+        scratch_shapes=[
+            pltpu.VMEM((batch, model_dim), BF16),
+            pltpu.VMEM((q_dim // TILE + 2, model_dim, TILE), BF16),
+            pltpu.VMEM((2, GROUP, local_kv, context, head_dim), BF16),
+            pltpu.VMEM((2, GROUP, local_kv, context, head_dim), BF16),
+            pltpu.VMEM((batch, 8, head_dim), F32),
+            pltpu.VMEM((batch, 8, head_dim), F32),
+            pltpu.VMEM((batch, 8, head_dim), F32),
+            pltpu.VMEM((items, 8, lanes), F32),
+            pltpu.VMEM((GROUP + 1, 8, lanes), F32),
+            pltpu.VMEM((GROUP + 1, 8, lanes), F32),
+            pltpu.VMEM((GROUP + 1, 8, head_dim), F32),
+            pltpu.SMEM((2, items), jnp.int32),
+            pltpu.SMEM((2, items), jnp.int32),
+            pltpu.SMEM((2,), jnp.int32),
+            dma, dma((q_dim // TILE + 2,)), dma((2,)), dma((2,)),
+        ],
+        compiler_params=pltpu.CompilerParams(vmem_limit_bytes=60 * 2 ** 20),
+        name="qkv_and_attend",
+    )(lengths, tokens, norm_gain.reshape(1, model_dim), cos_part, sin_part, k_cache, v_cache, w_query, w_key, w_value)
+
+
+def mlp_kernel(h_buf, tokens, o_buf, kv_buf, w_gate, w_up, w_down, w_out,
                y_out, key_out, value_out,
-               h_buf, x_buf, o_buf, kv_buf, w_buf, wo_buf, u_buf, part, from_sib, to_cross, from_cross, y_buf, kv_in, head_buf,
+               x_buf, w_buf, wo_buf, u_buf, part, from_sib, to_cross, from_cross, y_buf, kv_in, head_buf, new_buf,
                in_sem, w_sem, wo_sem, kv_send, kv_recv, s1_send, s1_recv, s2_send, s2_recv,
-               yc_send, yc_recv, ys_send, ys_recv, yr_send, yr_recv, out_sem):
+               yc_send, yc_recv, ys_send, ys_recv, yr_send, yr_recv, out_sem, new_sem):
     me = lax.axis_index('model')
     core = lax.rem(me, 2)
     chip = lax.div(me, 2)
@@ -70,7 +243,7 @@
     n_hid = width // TILE
     n_out = model_dim // TILE
     head_dim = head_buf.shape[2]
-    local_kv = kv_new.shape[2] // (2 * head_dim)
+    local_kv = kv_buf.shape[2] // (2 * head_dim)
 
     barrier = pltpu.get_barrier_semaphore()
     for peer in (sib, cross, diag):
@@ -86,17 +259,11 @@
         return pltpu.make_async_remote_copy(src_ref=src, dst_ref=dst, send_sem=send, recv_sem=recv,
                                             device_id={'model': peer}, device_id_type=MESH)
 
-    h_copy = pltpu.make_async_copy(normed, h_buf, in_sem.at[0])
-    h_copy.start()
     for pair in range(AHEAD):
         fetch(w_gate, pair, 2 * pair).start()
         fetch(w_up, pair, 2 * pair + 1).start()
-    x_copy = pltpu.make_async_copy(tokens.at[me], x_buf, in_sem.at[1])
-    o_copy = pltpu.make_async_copy(attended, o_buf, in_sem.at[2])
-    kv_copy = pltpu.make_async_copy(kv_new, kv_buf, in_sem.at[3])
-    for copy in (x_copy, o_copy, kv_copy):
-        copy.start()
-    h_copy.wait()
+    x_copy = pltpu.make_async_copy(tokens.at[me], x_buf, in_sem)
+    x_copy.start()
 
     def hidden_tile(j):
         slot = lax.rem(2 * j, SLOTS)
@@ -115,7 +282,6 @@
 
     wo_copy = pltpu.make_async_copy(w_out, wo_buf, wo_sem)
     wo_copy.start()
-    kv_copy.wait()
     pl.semaphore_wait(barrier, 3)
     kv_sends = []
     for n, peer in enumerate((sib, cross, diag)):
@@ -131,7 +297,6 @@
         fetch(w_down, tile + 1, slot + 1).start()
 
     x_copy.wait()
-    o_copy.wait()
     wo_copy.wait()
 
     def sib_send(c):
@@ -199,7 +364,8 @@
                     for g in range(local_kv):
                         start = (half * local_kv + g) * head_dim
                         head_buf[:, source * local_kv + g, :] = kv_in[source, :, start:start + head_dim].astype(F32)
-                out[...] = head_buf[...].astype(BF16)
+                new_buf[half] = head_buf[...].astype(BF16)
+                pltpu.make_async_copy(new_buf.at[half], out, new_sem.at[half]).start()
 
         @pl.when(i >= 6)
         def _():
@@ -210,6 +376,8 @@
 
     for send in kv_sends:
         send.wait_send()
+    for half, out in enumerate((key_out, value_out)):
+        pltpu.make_async_copy(new_buf.at[half], out, new_sem.at[half]).wait()
 
     @pl.loop(0, n_out)
     def _(c):
@@ -232,18 +400,16 @@
     dma = pltpu.SemaphoreType.DMA
     hbm = pl.BlockSpec(memory_space=pl.ANY)
     vmem = pl.BlockSpec(memory_space=pltpu.VMEM)
+    out = pl.BlockSpec(memory_space=pltpu.HBM)
     y, key_out, value_out = pl.pallas_call(
         mlp_kernel,
         out_shape=(jax.ShapeDtypeStruct((devices, rows, model_dim), BF16),
                    jax.ShapeDtypeStruct((rows, kv_heads, head_dim), BF16),
                    jax.ShapeDtypeStruct((rows, kv_heads, head_dim), BF16)),
-        in_specs=[hbm] * 8,
-        out_specs=(hbm, vmem, vmem),
+        in_specs=[vmem, hbm, vmem, vmem] + [hbm] * 4,
+        out_specs=(out, out, out),
         scratch_shapes=[
-            pltpu.VMEM((batch, model_dim), BF16),
             pltpu.VMEM((rows, model_dim), BF16),
-            pltpu.VMEM((batch, q_dim), BF16),
-            pltpu.VMEM((devices, rows, kv_width), BF16),
             pltpu.VMEM((SLOTS, model_dim, TILE), BF16),
             pltpu.VMEM((q_dim, model_dim), BF16),
             pltpu.VMEM((batch, width), BF16),
@@ -254,8 +420,9 @@
             pltpu.VMEM((n_out, devices, rows, TILE), BF16),
             pltpu.VMEM((devices, rows, kv_width), BF16),
             pltpu.VMEM((rows, kv_heads, head_dim), F32),
-            dma((4,)), dma((SLOTS,)), dma, dma((3,)), dma((3,)),
-        ] + [dma((n_out,))] * 11,
+            pltpu.VMEM((2, rows, kv_heads, head_dim), BF16),
+            dma, dma((SLOTS,)), dma, dma((3,)), dma((3,)),
+        ] + [dma((n_out,))] * 11 + [dma((2,))],
         compiler_params=pltpu.CompilerParams(collective_id=0, has_side_effects=True, vmem_limit_bytes=48 * 2 ** 20),
         name="mlp_and_sum",
     )(normed, tokens.reshape(devices, rows, model_dim), attended, kv_new.reshape(devices, rows, kv_width), w_gate, w_up, w_down, w_out)
@@ -266,22 +433,8 @@
     groups = mesh.shape['model']
 
     def local_step(tokens, lengths, k_cache, v_cache, norm_gain, w_query, w_key, w_value, w_out, w_gate, w_up, w_down):
-        batch = tokens.shape[0]
-        kv_heads = k_cache.shape[1]
-        head_dim = k_cache.shape[3]
-        local_heads = w_query.shape[1] // head_dim
-        local_kv = kv_heads // groups
-        me = lax.axis_index('model')
-        normed = rms_norm(tokens, norm_gain)
-        queries = apply_rope(jnp.dot(normed, w_query, preferred_element_type=F32).reshape(batch, local_heads, head_dim), lengths).astype(BF16)
-        wk = lax.dynamic_slice_in_dim(w_key, me * local_kv * head_dim, local_kv * head_dim, 1)
-        wv = lax.dynamic_slice_in_dim(w_value, me * local_kv * head_dim, local_kv * head_dim, 1)
-        key_new = apply_rope(jnp.dot(normed, wk, preferred_element_type=F32).reshape(batch, local_kv, head_dim), lengths).astype(BF16)
-        value_new = jnp.dot(normed, wv, preferred_element_type=F32).reshape(batch, local_kv, head_dim).astype(BF16)
-        key_rows = lax.dynamic_slice_in_dim(k_cache, me * local_kv, local_kv, 1)
-        value_rows = lax.dynamic_slice_in_dim(v_cache, me * local_kv, local_kv, 1)
-        attended = attend(queries, key_rows, value_rows, key_new, value_new, lengths)
-        kv_new = jnp.concatenate([key_new.reshape(batch, -1), value_new.reshape(batch, -1)], axis=1)
+        kv_heads, _, head_dim = k_cache.shape[1:]
+        normed, attended, kv_new = qkv_and_attend(tokens, lengths, k_cache, v_cache, norm_gain, w_query, w_key, w_value, groups)
         return mlp_and_sum(normed, tokens, attended, kv_new, w_gate, w_up, w_down, w_out, kv_heads, head_dim)
 
     in_specs = (P('replica', None), P('replica'), P('replica', None, None, None), P('replica', None, None, None), P(None), P(None, 'model'), P(None, None), P(None, None), P('model', None), P(None, 'model'), P(None, 'model'), P('model', None))

time: 89.4 us -> 75.3 us (0.84)
  matrix products: 37.3 us -> 0 us
  Pallas kernels: 39.8 us -> 65.5 us
  other arithmetic: 6.64 us -> 1.73 us
  local copies, waits for them, and re-layouts: 4.5 us -> 6.4 us
    dot_general x6 -> x0, matrix products: 37.3 us -> none  [the longest x1 14.9 us: attend(): jnp.einsum('bgrd,bgtd->bgrt', grouped, key_rows, preferred_element_type=F32)]
    pallas_call x0 -> x1, Pallas kernels: none -> 25.9 us  [qkv_and_attend(): pl.pallas_call(attend_kernel, out_shape=(jax.ShapeDtypeStruct((batch, mod...]
    reduce_sum x2 -> x0, other arithmetic: 3.24 us -> none  [the longest x1 1.86 us: attend(): total = jnp.sum(weights, axis=-1) + weight_new]
    convert_element_type x6 -> x1, other arithmetic: 2.63 us -> 0.66 us  [rope_tables(): angles = positions.astype(F32)[:, None] * inv_freq[None, :]]
    unnamed x9 -> x11, local copies, waits for them, and re-layouts: 3.39 us -> 5.1 us
    reshape x2 -> x1, local copies, waits for them, and re-layouts: 0.22 us -> 1.3 us  [qkv_and_attend(): norm_gain.reshape(1, model_dim)]
where the time goes in v2:
time: 75.3 us; the launch traced here: 74.3 us
  Pallas kernels  65.5 us (87%)
  local copies, waits for them, and re-layouts  6.4 us (8%)
  other arithmetic  1.73 us (2%)
    pallas_call x1, Pallas kernels, mlp_and_sum(): pl.pallas_call(mlp_kernel, out_shape=(jax.ShapeDtypeStruct((devices, rows...  39.6 us
    pallas_call x1, Pallas kernels, qkv_and_attend(): pl.pallas_call(attend_kernel, out_shape=(jax.ShapeDtypeStruct((batch, mod...  25.9 us
    unnamed x11, local copies, waits for them, and re-layouts  5.1 us

profile of v2, /device:TPU:0, one launch (start us, length us, event | category | flops | bytes accessed | tf_op | source)
XLA Modules:
  0.0 74.3 jit_solution(17252452007597593030)
XLA Ops:
  0.6 0.7 convert_element_type.3
  1.3 1.3 %reshape.24.gain = bf16[1,3072]{1,0:T(2,128)(2,1)} reshape(bf16[3072]{0:T(1024)(128)(2,1)} %param.16) | data formatting | bytes 12288 | tf_op jit(solution)/shard_map/reshape | solution.py:227
  2.6 0.3 fusion
  2.9 0.8 %pad_maximum_fusion = (f32[128,128]{1,0:T(8,128)}, f32[128,128]{1,0:T(8,128)}) fusion(f32[128,64]{1,0:T(8,128)S(1)} %get-tuple-element.17, f32[128,64]{1,0:T(8,128)S(1)} %get-tuple-element.16, f32[128,64]{1,0:T(8,128)S(1)} %get-tuple-element.15), kind=kLoop, calls=%fused_computation.2 | loop fusion | flops 32768 | bytes 229376 | tf_op jit(solution)/shard_map/concatenate | solution.py:33
  3.7 0.0 copy-start
  3.7 25.9 %qkv_and_attend.1 = (bf16[128,3072]{1,0:T(8,128)(2,1)}, bf16[128,768]{1,0:T(8,128)(2,1)}, bf16[128,512]{1,0:T(8,128)(2,1)}) custom-call(s32[128]{0:T(128)} %lengths.1, bf16[128,3072]{1,0:T(8,128)(2,1)} %tokens.1, bf16[1,3072]{1,0:T(2,128)(2,1)} %reshape.24.gain, f32[128,128]{1,0:T(8,128)} %get-tuple-element.18.cos_part, ...), custom_call_target="tpu_custom_call" | custom-call | tf_op jit(solution)/shard_map/qkv_and_attend/pallas_call | solution.py:201
  29.6 0.0 copy-done
  29.6 0.0 copy-start.1
  29.6 1.1 %copy-done.1 = bf16[128,3072]{1,0:T(8,128)(2,1)S(1)} copy-done((bf16[128,3072]{1,0:T(8,128)(2,1)S(1)}, bf16[128,3072]{1,0:T(8,128)(2,1)}, u32[]{:S(2)}) %copy-start.1) | copy-done | bytes 786456
  30.7 0.0 copy-start.2
  30.7 0.9 %copy-done.2 = bf16[128,768]{1,0:T(8,128)(2,1)S(1)} copy-done((bf16[128,768]{1,0:T(8,128)(2,1)S(1)}, bf16[128,768]{1,0:T(8,128)(2,1)}, u32[]{:S(2)}) %copy-start.2) | copy-done | bytes 196632
  31.6 0.0 copy-start.3
  31.6 0.9 %copy-done.3 = bf16[128,512]{1,0:T(8,128)(2,1)S(1)} copy-done((bf16[128,512]{1,0:T(8,128)(2,1)S(1)}, bf16[128,512]{1,0:T(8,128)(2,1)}, u32[]{:S(2)}) %copy-start.3) | copy-done | bytes 131096
  32.5 39.6 %mlp_and_sum.1 = (bf16[4,32,3072]{2,1,0:T(8,128)(2,1)S(1)}, bf16[32,8,128]{2,1,0:T(8,128)(2,1)S(1)}, bf16[32,8,128]{2,1,0:T(8,128)(2,1)S(1)}) custom-call(bf16[128,3072]{1,0:T(8,128)(2,1)S(1)} %copy-done.1, bf16[4,32,3072]{2,1,0:T(8,128)(2,1)S(1)} %bitcast.3, bf16[128,768]{1,0:T(8,128)(2,1)S(1)} %copy-done.2, bf16[4,32,512]{2,1,0:T(8,128)(2,1)S(1)} %bitcast.5, ...), custom_call_target="tpu_custom_call" | custom-call | tf_op jit(solution)/shard_map/mlp_and_sum/pallas_call | solution.py:404
  72.2 0.9 %copy.18 = bf16[128,3072]{1,0:T(8,128)(2,1)} copy(bf16[128,3072]{1,0:T(8,128)(2,1)S(1)} %bitcast.4) | data formatting | bytes 1572864
  73.1 0.6 copy.19
  73.7 0.6 copy.20
  (1 shorter events, 0.0 us)
Async XLA Ops:
  3.7 25.9 %copy-start = (bf16[128,3072]{1,0:T(8,128)(2,1)S(1)}, bf16[128,3072]{1,0:T(8,128)(2,1)}, u32[]{:S(2)}) copy-start(bf16[128,3072]{1,0:T(8,128)(2,1)} %tokens.1) | copy-start | bytes 2359300
  29.6 1.1 %copy-start.1 = (bf16[128,3072]{1,0:T(8,128)(2,1)S(1)}, bf16[128,3072]{1,0:T(8,128)(2,1)}, u32[]{:S(2)}) copy-start(bf16[128,3072]{1,0:T(8,128)(2,1)} %get-tuple-element.9.h_buf) | copy-start | bytes 2359300
  30.7 0.9 %copy-start.2 = (bf16[128,768]{1,0:T(8,128)(2,1)S(1)}, bf16[128,768]{1,0:T(8,128)(2,1)}, u32[]{:S(2)}) copy-start(bf16[128,768]{1,0:T(8,128)(2,1)} %get-tuple-element.10.o_buf) | copy-start | bytes 589828
  31.6 0.9 %copy-start.3 = (bf16[128,512]{1,0:T(8,128)(2,1)S(1)}, bf16[128,512]{1,0:T(8,128)(2,1)}, u32[]{:S(2)}) copy-start(bf16[128,512]{1,0:T(8,128)(2,1)} %get-tuple-element.11) | copy-start | bytes 393220
